TPU v7x, 32 devices: a whole 2x2x4 slice. The times are simulated.
32 devices in a mesh: dp: 8 (over y, x, core), mp: 4 (over z).
Axes of the slice: x: 2, y: 2, z: 4, core: 2. Of those that a mesh axis runs over, the one named last changes fastest.
Arguments:
- tokens: bfloat16 [5120, 768], P('dp'), may hold values from -6 to 6
- segment_ids: int32 [8, 640], P('dp'), may hold values from 0 to 3, never falling along the last dimension, each value on 1 to 320 neighbouring positions
- token_types: int32 [8, 640], P('dp'), may hold values 0 or 1
- q_weight: bfloat16 [4, 768, 768], P(None, None, 'mp'), may hold values from -0.21875 to 0.21875
- k_weight: bfloat16 [768, 768], P(None, 'mp'), may hold values from -0.21875 to 0.21875
- v_weight: bfloat16 [768, 768], P(None, 'mp'), may hold values from -0.21875 to 0.21875
- o_weight: bfloat16 [768, 768], P('mp'), may hold values from -2.5 to 2.5
- o_bias: float32 [768], replicated, may hold values from -1.5 to 1.5
- norm1_gain: float32 [768], replicated, may hold values from 0.25 to 1.75
- norm1_shift: float32 [768], replicated, may hold values from -1.5 to 1.5
- in_weight: bfloat16 [768, 3072], P(None, 'mp'), may hold values from -0.21875 to 0.21875
- in_bias: float32 [3072], P('mp'), may hold values from -1.5 to 1.5
- out_weight: bfloat16 [3072, 768], P('mp'), may hold values from -0.109375 to 0.109375
- out_bias: float32 [768], replicated, may hold values from -1.5 to 1.5
- norm2_gain: float32 [768], replicated, may hold values from 0.25 to 1.75
- norm2_shift: float32 [768], replicated, may hold values from -1.5 to 1.5
- cotangent: bfloat16 [5120, 768], P('dp'), may hold values from -6 to 6
Outputs:
- layer_out: bfloat16 [5120, 768], P('dp')
- tokens_grad: bfloat16 [5120, 768], P('dp')
- q_grad: float32 [4, 768, 768], P(None, 'dp', 'mp')
- k_grad: float32 [768, 768], P('dp', 'mp')
- v_grad: float32 [768, 768], P('dp', 'mp')
- o_grad: float32 [768, 768], P('mp', 'dp')
- o_bias_grad: float32 [768], replicated
- norm1_gain_grad: float32 [768], replicated
- norm1_shift_grad: float32 [768], replicated
- in_grad: float32 [768, 3072], P('dp', 'mp')
- in_bias_grad: float32 [3072], P('mp')
- out_grad: float32 [3072, 768], P('mp', 'dp')
- out_bias_grad: float32 [768], replicated
- norm2_gain_grad: float32 [768], replicated
- norm2_shift_grad: float32 [768], replicated
Inputs may be any that keep to these rules, and one draw needn't show every extreme that they name: `segment_ids`: a sequence's rows with equal ids form one run.
All inputs are finite; a program needn't handle non-finite values. No bound on the sum of `token_types` on one device may be relied on, other than what follows from the above.
Results may differ from a plain program's by a relative error of at most 0.019.
Values may be sent and summed in bfloat16 or wider, within the bound.
A program may use at most 128 MiB of HBM per device.

v0:
```python
import jax
import jax.numpy as jnp
from jax import lax
from jax.sharding import PartitionSpec as P

HD = 64
norm_epsilon = 1e-05


def layer_norm(inputs, gain, shift):
    average = jnp.mean(inputs, axis=-1, keepdims=True)
    centred = inputs - average
    spread = jnp.mean(centred * centred, axis=-1, keepdims=True)
    return centred * lax.rsqrt(spread + norm_epsilon) * gain + shift


def gelu_exact(inputs):
    return jax.nn.gelu(inputs, approximate=False)


def matmul(left, right):
    return jnp.dot(left, right, preferred_element_type=jnp.float32)


def local(
    tokens,
    segment_ids,
    token_types,
    q_weight,
    k_weight,
    v_weight,
    o_weight,
    o_bias,
    norm1_gain,
    norm1_shift,
    in_weight,
    in_bias,
    out_weight,
    out_bias,
    norm2_gain,
    norm2_shift,
    cotangent,
):
    row_count = tokens.shape[0]
    groups, length = segment_ids.shape
    local_width = k_weight.shape[1]
    head_count = local_width // HD
    score_scale = HD ** (-0.5)
    entity = token_types == 1
    chooser = entity[:, :, None, None]
    key_entity = entity[:, None, None, :]
    same_doc = (segment_ids[:, :, None] == segment_ids[:, None, :])[:, None]
    share_rows = row_count // lax.axis_size("mp")
    row_offset = lax.axis_index("mp") * share_rows
    queries = jnp.einsum(
        "rd,tdc->trc", tokens, q_weight, preferred_element_type=jnp.float32
    ).astype(jnp.bfloat16)
    keys = matmul(tokens, k_weight).astype(jnp.bfloat16)
    values = matmul(tokens, v_weight).astype(jnp.bfloat16)
    query_four = queries.reshape(4, groups, length, head_count, HD)
    query_word = jnp.where(chooser, query_four[2], query_four[0])
    query_ent = jnp.where(chooser, query_four[3], query_four[1])
    key_heads = keys.reshape(groups, length, head_count, HD)
    value_heads = values.reshape(groups, length, head_count, HD)

    def scores_now():
        raw_word = jnp.einsum(
            "gqhc,gkhc->ghqk", query_word, key_heads, preferred_element_type=jnp.float32
        )
        raw_ent = jnp.einsum(
            "gqhc,gkhc->ghqk", query_ent, key_heads, preferred_element_type=jnp.float32
        )
        raw_all = jnp.where(key_entity, raw_ent, raw_word)
        return jnp.where(same_doc, raw_all * score_scale, -1000000000.0)

    scores = scores_now()
    highest = jnp.max(scores, axis=-1, keepdims=True)
    log_total = highest + jnp.log(jnp.sum(jnp.exp(scores - highest), axis=-1, keepdims=True))
    attention_low = jnp.exp(scores - log_total).astype(jnp.bfloat16)
    mixed = jnp.einsum(
        "ghqk,gkhc->gqhc", attention_low, value_heads, preferred_element_type=jnp.float32
    )
    mixed = mixed.reshape(row_count, local_width).astype(jnp.bfloat16)
    token_wide = tokens.astype(jnp.float32)
    branch = lax.psum(matmul(mixed, o_weight), "mp") + o_bias
    hidden, norm1_pull = jax.vjp(layer_norm, token_wide + branch, norm1_gain, norm1_shift)
    hidden_low = hidden.astype(jnp.bfloat16)
    inner_pre = matmul(hidden_low, in_weight) + in_bias
    activated, gelu_pull = jax.vjp(gelu_exact, inner_pre)
    activated_low = activated.astype(jnp.bfloat16)
    ffn_out = (
        lax.psum(matmul(activated_low, out_weight).astype(jnp.bfloat16), "mp").astype(jnp.float32)
        + out_bias
    )
    result, norm2_pull = jax.vjp(layer_norm, hidden + ffn_out, norm2_gain, norm2_shift)
    layer_out = result.astype(jnp.bfloat16)
    d_res2, d_gain2, d_shift2 = norm2_pull(cotangent.astype(jnp.float32))
    d_out_bias = jnp.sum(d_res2, axis=0)
    grad_ffn = d_res2.astype(jnp.bfloat16)
    d_out_weight = matmul(activated_low.T, grad_ffn)
    (d_inner,) = gelu_pull(matmul(grad_ffn, out_weight.T))
    d_in_bias = jnp.sum(d_inner, axis=0)
    inner_low = d_inner.astype(jnp.bfloat16)
    d_in_weight = matmul(hidden_low.T, inner_low)
    d_hidden = d_res2 + lax.psum(matmul(inner_low, in_weight.T).astype(jnp.bfloat16), "mp").astype(
        jnp.float32
    )
    d_res1, d_gain1, d_shift1 = norm1_pull(d_hidden)
    d_o_bias = jnp.sum(d_res1, axis=0)
    grad_branch = d_res1.astype(jnp.bfloat16)
    d_o_weight = matmul(mixed.T, grad_branch)
    d_mixed = matmul(grad_branch, o_weight.T).astype(jnp.bfloat16)
    mixed_heads = d_mixed.reshape(groups, length, head_count, HD)
    attention = jnp.exp(scores_now() - log_total)
    d_probs = jnp.einsum(
        "gqhc,gkhc->ghqk", mixed_heads, value_heads, preferred_element_type=jnp.float32
    )
    d_values = jnp.einsum(
        "ghqk,gqhc->gkhc",
        attention.astype(jnp.bfloat16),
        mixed_heads,
        preferred_element_type=jnp.float32,
    )
    row_delta = jnp.sum(attention * d_probs, axis=-1, keepdims=True)
    d_raw = (attention * (d_probs - row_delta) * score_scale).astype(jnp.bfloat16)
    nothing = jnp.zeros_like(d_raw)
    raw_word = jnp.where(key_entity, nothing, d_raw)
    raw_ent = jnp.where(key_entity, d_raw, nothing)
    d_query_word = jnp.einsum(
        "ghqk,gkhc->gqhc", raw_word, key_heads, preferred_element_type=jnp.float32
    )
    d_query_ent = jnp.einsum(
        "ghqk,gkhc->gqhc", raw_ent, key_heads, preferred_element_type=jnp.float32
    )
    d_keys = jnp.einsum(
        "ghqk,gqhc->gkhc", raw_word, query_word, preferred_element_type=jnp.float32
    ) + jnp.einsum("ghqk,gqhc->gkhc", raw_ent, query_ent, preferred_element_type=jnp.float32)
    empty_rows = jnp.zeros_like(d_query_word)
    d_queries = (
        jnp.stack(
            [
                jnp.where(chooser, empty_rows, d_query_word),
                jnp.where(chooser, empty_rows, d_query_ent),
                jnp.where(chooser, d_query_word, empty_rows),
                jnp.where(chooser, d_query_ent, empty_rows),
            ]
        )
        .reshape(4, row_count, local_width)
        .astype(jnp.bfloat16)
    )
    d_keys_low = d_keys.reshape(row_count, local_width).astype(jnp.bfloat16)
    d_values_low = d_values.reshape(row_count, local_width).astype(jnp.bfloat16)
    d_q_weight = jnp.einsum("rd,trc->tdc", tokens, d_queries, preferred_element_type=jnp.float32)
    d_k_weight = matmul(tokens.T, d_keys_low)
    d_v_weight = matmul(tokens.T, d_values_low)
    res_rows = lax.dynamic_slice_in_dim(d_res1, row_offset, share_rows, 0)
    total = jnp.einsum("trc,tdc->rd", d_queries, q_weight, preferred_element_type=jnp.float32)
    grad_rows = (
        res_rows
        + lax.psum_scatter(
            (total + matmul(d_keys_low, k_weight.T) + matmul(d_values_low, v_weight.T)).astype(
                jnp.bfloat16
            ),
            "mp",
            scatter_dimension=0,
            tiled=True,
        ).astype(jnp.float32)
    ).astype(jnp.bfloat16)
    tokens_grad = lax.all_gather(grad_rows, "mp", axis=0, tiled=True)
    d_q_weight, d_k_weight, d_v_weight, d_o_weight, d_in_weight, d_out_weight = (
        lax.psum_scatter(d_q_weight, "dp", scatter_dimension=1, tiled=True),
        lax.psum_scatter(d_k_weight, "dp", scatter_dimension=0, tiled=True),
        lax.psum_scatter(d_v_weight, "dp", scatter_dimension=0, tiled=True),
        lax.psum_scatter(d_o_weight, "dp", scatter_dimension=1, tiled=True),
        lax.psum_scatter(d_in_weight, "dp", scatter_dimension=0, tiled=True),
        lax.psum_scatter(d_out_weight, "dp", scatter_dimension=1, tiled=True),
    )
    d_o_bias, d_gain1, d_shift1, d_in_bias, d_out_bias, d_gain2, d_shift2 = lax.psum(
        (d_o_bias, d_gain1, d_shift1, d_in_bias, d_out_bias, d_gain2, d_shift2), "dp"
    )
    return (
        layer_out,
        tokens_grad,
        d_q_weight,
        d_k_weight,
        d_v_weight,
        d_o_weight,
        d_o_bias,
        d_gain1,
        d_shift1,
        d_in_weight,
        d_in_bias,
        d_out_weight,
        d_out_bias,
        d_gain2,
        d_shift2,
    )


def solution(mesh):
    return jax.shard_map(
        local,
        mesh=mesh,
        in_specs=(
            P("dp", None),
            P("dp", None),
            P("dp", None),
            P(None, None, "mp"),
            P(None, "mp"),
            P(None, "mp"),
            P("mp", None),
            P(),
            P(),
            P(),
            P(None, "mp"),
            P("mp"),
            P("mp", None),
            P(),
            P(),
            P(),
            P("dp", None),
        ),
        out_specs=(
            P("dp", None),
            P("dp", None),
            P(None, "dp", "mp"),
            P("dp", "mp"),
            P("dp", "mp"),
            P("mp", "dp"),
            P(),
            P(),
            P(),
            P("dp", "mp"),
            P("mp"),
            P("mp", "dp"),
            P(),
            P(),
            P(),
        ),
        check_vma=False,
    )
```

profile of v0, /device:TPU:0, one launch (start us, length us, event | category | flops | bytes accessed | tf_op | source)
XLA Modules:
  0.0 547.0 jit_solution(5020968630286662695)
XLA Ops:
  12.0 2.4 fusion.19
  22.2 84.7 %all-reduce.5.cloned.1.call-done = f32[640,768]{1,0:T(8,128)} async-done(((f32[640,768]{1,0:T(8,128)}), f32[640,768]{1,0:T(8,128)}) %all-reduce.5.cloned.1.call-update) | async-done | bytes 1966096 | tf_op jit(solution)/shard_map/psum | solution.py:85
  106.9 2.1 fusion.75
  109.7 6.5 %multiply_convert_fusion.1 = (bf16[640,768]{1,0:T(8,128)(2,1)S(1)}, f32[640,768]{1,0:T(8,128)}, f32[640,768]{1,0:T(8,128)}) fusion(f32[768]{0:T(1024)S(1)} %copy-done.36, bf16[768,768]{1,0:T(8,128)(2,1)S(1)} %copy-done, f32[640,768]{1,0:T(8,128)S(1)} %get-tuple-element.70, f32[768]{0:T(1024)S(1)} %copy-done.31, f32[768]{0:T(1024)S(1)} %copy-done.27, ...), kind=kOutput, calls=%fused_computation.32 | convolution fusion | flops 789872640 | bytes 8075264 | tf_op jit(solution)/shard_map/dot_general | solution.py:22
  117.2 1.9 convolution_convert_fusion.1
  119.6 48.5 %all-reduce.7.cloned.1.call-done = bf16[640,768]{1,0:T(8,128)(2,1)} async-done(((bf16[640,768]{1,0:T(8,128)(2,1)}), bf16[640,768]{1,0:T(8,128)(2,1)}) %all-reduce.7.cloned.1.call-update) | async-done | bytes 983056 | tf_op jit(solution)/shard_map/psum | solution.py:92
  168.2 1.9 fusion.73
  177.6 1.9 convolution_convert_fusion
  179.6 49.1 %all-reduce.9.cloned.1.call-done = bf16[640,768]{1,0:T(8,128)(2,1)} async-done(((bf16[640,768]{1,0:T(8,128)(2,1)}), bf16[640,768]{1,0:T(8,128)(2,1)}) %all-reduce.9.cloned.1.call-update) | async-done | bytes 983056 | tf_op jit(solution)/shard_map/psum | solution.py:105
  228.7 3.1 multiply_reduce_fusion.1
  235.9 3.4 convolution_convert_fusion.3
  239.3 3.1 fusion.82
  242.4 9.7 %fusion.21 = f32[3,64,640]{2,1,0:T(8,128)} fusion(pred[640]{0:T(1024)(128)(4,1)S(1)} %compare_reduce_fusion, f32[3,640,640]{1,2,0:T(8,128)} %fusion.82, f32[3,640,640]{1,2,0:T(8,128)} %copy-done.2, f32[3,640]{1,0:T(4,128)S(1)} %log_add_fusion, bf16[640,3,64]{0,2,1:T(8,128)(2,1)S(1)} %bitcast.122, bf16[640,3,64]{0,2,1:T(8,128)(2,1)S(1)} %bitcast.120), kind=kOutput, calls=%fused_computation.69 | convolution fusion | flops 167242240 | bytes 10821760 | tf_op jit(solution)/shard_map/ghqk,gqhc->gkhc/dot_general | solution.py:135
  252.1 9.6 %convolution_bitcast_fusion.4 = bf16[1,3,64,640]{3,2,1,0:T(8,128)(2,1)} fusion(bf16[640,3,64]{0,2,1:T(8,128)(2,1)S(1)} %bitcast.104, pred[640]{0:T(1024)(128)(4,1)S(1)} %compare_reduce_fusion, f32[3,640,640]{1,2,0:T(8,128)} %fusion.82, f32[3,640,640]{1,2,0:T(8,128)} %copy-done.2, f32[3,640]{1,0:T(4,128)S(1)} %log_add_fusion), kind=kOutput, calls=%fused_computation.60 | convolution fusion | flops 167119360 | bytes 10330240 | tf_op jit(solution)/shard_map/ghqk,gkhc->gqhc/dot_general | solution.py:132
  263.7 9.3 %fusion.20 = bf16[3,64,640]{2,1,0:T(8,128)(2,1)S(1)} fusion(f32[3,64,640]{2,1,0:T(8,128)} %fusion.21, pred[640]{0:T(1024)(128)(4,1)S(1)} %compare_reduce_fusion, f32[3,640,640]{1,2,0:T(8,128)} %fusion.82, f32[3,640,640]{1,2,0:T(8,128)} %copy-done.2, f32[3,640]{1,0:T(4,128)S(1)} %log_add_fusion, bf16[640,3,64]{0,2,1:T(8,128)(2,1)} %bitcast.118, ...), kind=kOutput, calls=%fused_computation.63 | convolution fusion | flops 167488000 | bytes 11067520 | tf_op jit(solution)/shard_map/ghqk,gqhc->gkhc/dot_general | solution.py:137
  272.9 9.9 %select_convert_fusion.3 = (bf16[1,3,64,640]{3,2,1,0:T(8,128)(2,1)}, bf16[1,3,64,640]{3,2,1,0:T(8,128)(2,1)}, bf16[1,3,64,640]{3,2,1,0:T(8,128)(2,1)}, bf16[1,3,64,640]{3,2,1,0:T(8,128)(2,1)}) fusion(pred[640]{0:T(1024)(128)(4,1)S(1)} %compare_reduce_fusion, bf16[1,3,64,640]{3,2,1,0:T(8,128)(2,1)} %convolution_bitcast_fusion.4, ...), kind=kOutput, calls=%fused_computation.79 | convolution fusion | flops 167610880 | bytes 11313280 | tf_op jit(solution)/shard_map/ghqk,gkhc->gqhc/dot_general | solution.py:129
  284.5 3.6 fusion.12
  288.2 3.9 convolution_bitcast_fusion
  292.1 4.5 copy.56
  296.6 4.7 reshape.292
  302.6 2.2 copy.60
  304.9 2.2 convolution_bitcast_fusion.3
  307.1 2.4 copy.58
  309.6 4.2 fusion.64
  315.0 2.8 fusion.44
  317.8 24.7 %all-reduce = (f32[768]{0:T(1024)}, f32[768]{0:T(1024)}, f32[768]{0:T(1024)}, f32[768]{0:T(1024)}, f32[768]{0:T(1024)}, /*index=5*/f32[768]{0:T(1024)}, f32[768]{0:T(1024)}) all-reduce(f32[768]{0:T(1024)S(1)} %get-tuple-element.59, f32[768]{0:T(1024)S(1)} %get-tuple-element.45, ...), channel_id=1, replica_groups=mesh['dp'=8,'mp'=4] {'dp'}, use_global_device_ids=true, to_apply=%region_20.21 | all-reduce | flops 5376 | bytes 43008 | tf_op jit(solution)/shard_map/psum | solution.py:178
  345.3 19.9 %all_gather.3 = bf16[640,768]{1,0:T(8,128)(2,1)S(1)} all-gather(bf16[160,768]{1,0:T(8,128)(2,1)S(1)} %add_convert_fusion.2), channel_id=1, replica_groups=mesh['dp'=8,'mp'=4] {'mp'}, dimensions={0}, use_global_device_ids=true | all-gather | bytes 1228800 | tf_op jit(solution)/shard_map/all_gather | solution.py:169
  365.2 3.9 reduce-scatter.22.cloned.1.call-done
  371.2 36.6 %reduce-scatter.26.cloned.1.call-done = f32[96,192]{1,0:T(8,128)} async-done(((f32[768,192]{1,0:T(8,128)}), f32[96,192]{1,0:T(8,128)}) %reduce-scatter.26.cloned.1.call-update) | async-done | bytes 73744
  407.8 38.7 %reduce-scatter.24.cloned.1.call-done = f32[96,192]{1,0:T(8,128)} async-done(((f32[768,192]{1,0:T(8,128)}), f32[96,192]{1,0:T(8,128)}) %reduce-scatter.24.cloned.1.call-update) | async-done | bytes 73744
  446.5 46.3 %reduce-scatter.20.cloned.1.call-done = f32[768,96]{0,1:T(8,128)} async-done(((f32[768,768]{0,1:T(8,128)}), f32[768,96]{0,1:T(8,128)}) %reduce-scatter.20.cloned.1.call-update) | async-done | bytes 294928 | tf_op jit(solution)/shard_map/reduce_scatter | solution.py:176
  492.8 46.1 %reduce-scatter.18.cloned.1.call-done = f32[96,768]{1,0:T(8,128)} async-done(((f32[768,768]{1,0:T(8,128)}), f32[96,768]{1,0:T(8,128)}) %reduce-scatter.18.cloned.1.call-update) | async-done | bytes 294928 | tf_op jit(solution)/shard_map/reduce_scatter | solution.py:175
  (149 shorter events, 38.3 us)
Async XLA Ops:
  7.2 102.2 %copy-start = (bf16[768,768]{1,0:T(8,128)(2,1)S(1)}, bf16[768,768]{1,0:T(8,128)(2,1)}, u32[]{:S(2)}) copy-start(bf16[768,768]{1,0:T(8,128)(2,1)} %param.27) | copy-start | bytes 3538948
  7.2 4.8 copy-start.3
  7.2 4.5 copy-start.33
  7.2 99.6 %all-reduce.5.cloned.1.call-start = ((), (), s32[]{:S(2)}) async-start(), calls=%async_computation.7 | async-start | bytes 3932160 | tf_op jit(solution)/shard_map/psum | solution.py:85
  9.8 5.6 %copy-start.10 = (bf16[640,192]{0,1:T(8,128)(2,1)}, bf16[640,192]{0,1:T(8,128)(2,1)S(1)}, u32[]{:S(2)}) copy-start(bf16[640,192]{0,1:T(8,128)(2,1)S(1)} %convolution_convert_fusion.6) | copy-start | bytes 737284
  11.7 6.1 %copy-start.12 = (bf16[640,192]{0,1:T(8,128)(2,1)}, bf16[640,192]{0,1:T(8,128)(2,1)S(1)}, u32[]{:S(2)}) copy-start(bf16[640,192]{0,1:T(8,128)(2,1)S(1)} %convolution_convert_fusion.7) | copy-start | bytes 737284
  20.3 86.6 %copy-start.29 = (f32[768]{0:T(1024)S(1)}, f32[768]{0:T(1024)}, u32[]{:S(2)}) copy-start(f32[768]{0:T(1024)} %param.24) | copy-start | bytes 9220
  22.1 146.0 %all-reduce.7.cloned.1.call-start = ((), (), s32[]{:S(2)}) async-start(), calls=%async_computation.8 | async-start | bytes 1966080 | tf_op jit(solution)/shard_map/psum | solution.py:92
  109.7 7.5 %copy-start.34 = (bf16[768,768]{1,0:T(8,128)(2,1)S(1)}, bf16[768,768]{1,0:T(8,128)(2,1)}, u32[]{:S(2)}) copy-start(bf16[768,768]{1,0:T(8,128)(2,1)} %param.29) | copy-start | bytes 3538948
  117.2 50.9 %copy-start.30 = (f32[768]{0:T(1024)S(1)}, f32[768]{0:T(1024)}, u32[]{:S(2)}) copy-start(f32[768]{0:T(1024)} %param.30) | copy-start | bytes 9220
  119.1 109.6 %all-reduce.9.cloned.1.call-start = ((), (), s32[]{:S(2)}) async-start(), calls=%async_computation.9 | async-start | bytes 1966080 | tf_op jit(solution)/shard_map/psum | solution.py:105
  172.2 2.9 copy-start.44
  174.0 2.6 copy-start.6
  179.5 163.0 %reduce-scatter.28.cloned.1.call-start = ((), (), s32[]{:S(2)}) async-start(), calls=%async_computation.16 | async-start | bytes 884736
  228.7 3.1 copy-start.7
  228.7 3.1 copy-start.8
  235.9 3.4 copy-start.13
  239.3 3.1 copy-start.24
  239.3 3.1 copy-start.26
  242.4 9.7 %copy-start.11 = (bf16[640,192]{0,1:T(8,128)(2,1)S(1)}, bf16[640,192]{0,1:T(8,128)(2,1)}, u32[]{:S(2)}) copy-start(bf16[640,192]{0,1:T(8,128)(2,1)} %copy-done.10) | copy-start | bytes 737284
  252.1 9.8 %copy-start.17 = (bf16[768,192]{0,1:T(8,128)(2,1)S(1)}, bf16[768,192]{0,1:T(8,128)(2,1)}, u32[]{:S(2)}) copy-start(bf16[768,192]{0,1:T(8,128)(2,1)} %param.22) | copy-start | bytes 884740
  261.7 82.4 %reduce-scatter.16.cloned.1.call-start = ((), (), s32[]{:S(2)}) async-start(), calls=%async_computation.10 | async-start | bytes 1228800 | tf_op jit(solution)/shard_map/reduce_scatter | solution.py:160
  272.9 9.9 %copy-start.19 = (bf16[3,64,640]{2,1,0:T(8,128)(2,1)}, bf16[3,64,640]{2,1,0:T(8,128)(2,1)S(1)}, u32[]{:S(2)}) copy-start(bf16[3,64,640]{2,1,0:T(8,128)(2,1)S(1)} %fusion.20) | copy-start | bytes 737284
  272.9 9.9 %copy-start.18 = (bf16[768,192]{0,1:T(8,128)(2,1)S(1)}, bf16[768,192]{0,1:T(8,128)(2,1)}, u32[]{:S(2)}) copy-start(bf16[768,192]{0,1:T(8,128)(2,1)} %param.21) | copy-start | bytes 884740
  284.5 3.7 copy-start.4
  288.1 81.0 %reduce-scatter.22.cloned.1.call-start = ((), (), s32[]{:S(2)}) async-start(), calls=%async_computation.13 | async-start | bytes 2654208
  301.3 106.5 %reduce-scatter.26.cloned.1.call-start = ((), (), s32[]{:S(2)}) async-start(), calls=%async_computation.15 | async-start | bytes 884736
  304.8 141.7 %reduce-scatter.24.cloned.1.call-start = ((), (), s32[]{:S(2)}) async-start(), calls=%async_computation.14 | async-start | bytes 884736
  307.1 2.4 copy-start.40
  309.5 183.3 %reduce-scatter.20.cloned.1.call-start = ((), (), s32[]{:S(2)}) async-start(), calls=%async_computation.12 | async-start | bytes 2654208 | tf_op jit(solution)/shard_map/reduce_scatter | solution.py:176
  313.8 225.2 %reduce-scatter.18.cloned.1.call-start = ((), (), s32[]{:S(2)}) async-start(), calls=%async_computation.11 | async-start | bytes 2654208 | tf_op jit(solution)/shard_map/reduce_scatter | solution.py:175
  345.3 194.6 %copy-start.1 = (bf16[768,768]{1,0:T(8,128)(2,1)S(1)}, bf16[768,768]{1,0:T(8,128)(2,1)}, u32[]{:S(2)}) copy-start(bf16[768,768]{1,0:T(8,128)(2,1)} %param.27) | copy-start | bytes 3538948
  (23 other events, 29.0 us)
Sparse Core Ops, SparseCore 0:
  22.2 84.5 all-reduce.4
  119.2 48.8 all-reduce.6
  179.6 49.0 all-reduce.8
  261.8 34.1 reduce-scatter.27
  298.7 26.2 reduce-scatter.15
  328.2 40.9 reduce-scatter.21
  372.9 34.9 reduce-scatter.25
  411.6 34.9 reduce-scatter.23
  450.5 42.3 reduce-scatter.19
  496.6 42.3 reduce-scatter.17
where the time goes:
time: 554 us; the launch traced here: 547 us
  waiting for transfers between devices  354 us (64%)
  matrix products  90 us (16%)
  blocking collectives  44.6 us (8%)
  local copies, waits for them, and re-layouts  27.3 us (5%)
  between operations  14.9 us (3%)
  other arithmetic  14.8 us (3%)
    psum x1, waiting for transfers between devices, local(): branch = lax.psum(matmul(mixed, o_weight), 'mp') + o_bias  84.7 us
    unnamed x14, waiting for transfers between devices  79.4 us
    psum x1, waiting for transfers between devices, local(): lax.psum(matmul(inner_low, in_weight.T).astype(jnp.bfloat16), 'mp')  49.1 us
    psum x1, waiting for transfers between devices, local(): lax.psum(matmul(activated_low, out_weight).astype(jnp.bfloat16), 'mp')  48.5 us
    reduce_scatter x1, waiting for transfers between devices, local(): lax.psum_scatter(d_out_weight, 'dp', scatter_dimension=1, tiled=True)  46.3 us
    reduce_scatter x1, waiting for transfers between devices, local(): lax.psum_scatter(d_in_weight, 'dp', scatter_dimension=0, tiled=True)  46.1 us
    dot_general x14, matrix products, matmul(): return jnp.dot(left, right, preferred_element_type=jnp.float32)  30.4 us
    unnamed x98, local copies, waits for them, and re-layouts  27.2 us
  transfers between devices with their start and end apart: 10, of which 8 were waited for; matrix products, arithmetic and copies ran while one was open for 11% of the time, Pallas kernels for 0%

commit v1 on v0

--- a/solution.py
+++ b/solution.py
@@ -2,6 +2,7 @@
 import jax.numpy as jnp
 from jax import lax
 from jax.sharding import PartitionSpec as P
+from jax.lax import all_gather
 
 HD = 64
 norm_epsilon = 1e-05
@@ -82,7 +83,8 @@
     )
     mixed = mixed.reshape(row_count, local_width).astype(jnp.bfloat16)
     token_wide = tokens.astype(jnp.float32)
-    branch = lax.psum(matmul(mixed, o_weight), "mp") + o_bias
+    see_columns = lambda mat: all_gather(mat, "mp").sum(axis=0)
+    branch = see_columns(matmul(mixed, o_weight)) + o_bias
     hidden, norm1_pull = jax.vjp(layer_norm, token_wide + branch, norm1_gain, norm1_shift)
     hidden_low = hidden.astype(jnp.bfloat16)
     inner_pre = matmul(hidden_low, in_weight) + in_bias

time: 554 us -> 618 us (1.12)
  waiting for transfers between devices: 354 us -> 413 us
    all_gather x0 -> x1, waiting for transfers between devices: none -> 144 us  [local(): see_columns = lambda mat: all_gather(mat, 'mp').sum(axis=0)]
    psum x1 -> x0, waiting for transfers between devices: 84.7 us -> none  [local(): branch = lax.psum(matmul(mixed, o_weight), 'mp') + o_bias]
  transfers between devices with their start and end apart: 10 -> 10, of which waited for: 8 -> 8; matrix products, arithmetic and copies ran while one was open for 11% -> 10% of each run, Pallas kernels for 0% -> 0%
where the time goes in v1:
time: 618 us; the launch traced here: 610 us
  waiting for transfers between devices  413 us (67%)
  matrix products  89.8 us (15%)
  blocking collectives  44.5 us (7%)
  local copies, waits for them, and re-layouts  27.1 us (4%)
  other arithmetic  20.1 us (3%)
  between operations  14.9 us (2%)
    all_gather x1, waiting for transfers between devices, local(): see_columns = lambda mat: all_gather(mat, 'mp').sum(axis=0)  144 us
    unnamed x14, waiting for transfers between devices  79.5 us
    psum x1, waiting for transfers between devices, local(): lax.psum(matmul(inner_low, in_weight.T).astype(jnp.bfloat16), 'mp')  49.1 us
    psum x1, waiting for transfers between devices, local(): lax.psum(matmul(activated_low, out_weight).astype(jnp.bfloat16), 'mp')  47.7 us
    reduce_scatter x1, waiting for transfers between devices, local(): lax.psum_scatter(d_out_weight, 'dp', scatter_dimension=1, tiled=True)  46.3 us
    reduce_scatter x1, waiting for transfers between devices, local(): lax.psum_scatter(d_in_weight, 'dp', scatter_dimension=0, tiled=True)  46.1 us
    dot_general x14, matrix products, matmul(): return jnp.dot(left, right, preferred_element_type=jnp.float32)  30.3 us
    unnamed x98, local copies, waits for them, and re-layouts  27 us
  transfers between devices with their start and end apart: 10, of which 8 were waited for; matrix products, arithmetic and copies ran while one was open for 10% of the time, Pallas kernels for 0%

profile of v1, /device:TPU:0, one launch (start us, length us, event | category | flops | bytes accessed | tf_op | source)
XLA Modules:
  0.0 610.3 jit_solution(2320562929234718520)
XLA Ops:
  12.0 2.4 fusion.19
  22.1 143.9 %all-gather.3.cloned.1.call-done = f32[2560,768]{1,0:T(8,128)} async-done(((f32[640,768]{1,0:T(8,128)}), f32[2560,768]{1,0:T(8,128)}) %all-gather.3.cloned.1.call-update) | async-done | bytes 7864336 | tf_op jit(solution)/shard_map/all_gather | solution.py:86
  166.0 5.3 reduce_sum.160
  171.2 2.1 fusion.75
  174.1 6.5 %multiply_convert_fusion.1 = (bf16[640,768]{1,0:T(8,128)(2,1)S(1)}, f32[640,768]{1,0:T(8,128)}, f32[640,768]{1,0:T(8,128)}) fusion(f32[768]{0:T(1024)S(1)} %copy-done.36, bf16[768,768]{1,0:T(8,128)(2,1)S(1)} %copy-done, f32[640,768]{1,0:T(8,128)S(1)} %get-tuple-element.70, f32[768]{0:T(1024)S(1)} %copy-done.31, f32[768]{0:T(1024)S(1)} %copy-done.27, ...), kind=kOutput, calls=%fused_computation.32 | convolution fusion | flops 789872640 | bytes 8075264 | tf_op jit(solution)/shard_map/dot_general | solution.py:23
  183.9 47.7 %all-reduce.4.cloned.1.call-done = bf16[640,768]{1,0:T(8,128)(2,1)} async-done(((bf16[640,768]{1,0:T(8,128)(2,1)}), bf16[640,768]{1,0:T(8,128)(2,1)}) %all-reduce.4.cloned.1.call-update) | async-done | bytes 983056 | tf_op jit(solution)/shard_map/psum | solution.py:94
  231.6 1.9 fusion.73
  241.1 1.9 convolution_convert_fusion
  243.0 49.1 %all-reduce.6.cloned.1.call-done = bf16[640,768]{1,0:T(8,128)(2,1)} async-done(((bf16[640,768]{1,0:T(8,128)(2,1)}), bf16[640,768]{1,0:T(8,128)(2,1)}) %all-reduce.6.cloned.1.call-update) | async-done | bytes 983056 | tf_op jit(solution)/shard_map/psum | solution.py:107
  292.2 3.1 multiply_reduce_fusion.1
  299.3 3.4 convolution_convert_fusion.3
  302.7 3.0 fusion.82
  305.7 9.7 %fusion.21 = f32[3,64,640]{2,1,0:T(8,128)} fusion(pred[640]{0:T(1024)(128)(4,1)S(1)} %compare_reduce_fusion, f32[3,640,640]{1,2,0:T(8,128)} %fusion.82, f32[3,640,640]{1,2,0:T(8,128)} %copy-done.2, f32[3,640]{1,0:T(4,128)S(1)} %log_add_fusion, bf16[640,3,64]{0,2,1:T(8,128)(2,1)S(1)} %bitcast.124, bf16[640,3,64]{0,2,1:T(8,128)(2,1)S(1)} %bitcast.122), kind=kOutput, calls=%fused_computation.69 | convolution fusion | flops 167242240 | bytes 10821760 | tf_op jit(solution)/shard_map/ghqk,gqhc->gkhc/dot_general | solution.py:137
  315.4 9.6 %convolution_bitcast_fusion.4 = bf16[1,3,64,640]{3,2,1,0:T(8,128)(2,1)} fusion(bf16[640,3,64]{0,2,1:T(8,128)(2,1)S(1)} %bitcast.106, pred[640]{0:T(1024)(128)(4,1)S(1)} %compare_reduce_fusion, f32[3,640,640]{1,2,0:T(8,128)} %fusion.82, f32[3,640,640]{1,2,0:T(8,128)} %copy-done.2, f32[3,640]{1,0:T(4,128)S(1)} %log_add_fusion), kind=kOutput, calls=%fused_computation.60 | convolution fusion | flops 167119360 | bytes 10330240 | tf_op jit(solution)/shard_map/ghqk,gkhc->gqhc/dot_general | solution.py:134
  327.0 9.3 %fusion.20 = bf16[3,64,640]{2,1,0:T(8,128)(2,1)S(1)} fusion(f32[3,64,640]{2,1,0:T(8,128)} %fusion.21, pred[640]{0:T(1024)(128)(4,1)S(1)} %compare_reduce_fusion, f32[3,640,640]{1,2,0:T(8,128)} %fusion.82, f32[3,640,640]{1,2,0:T(8,128)} %copy-done.2, f32[3,640]{1,0:T(4,128)S(1)} %log_add_fusion, bf16[640,3,64]{0,2,1:T(8,128)(2,1)} %bitcast.120, ...), kind=kOutput, calls=%fused_computation.63 | convolution fusion | flops 167488000 | bytes 11067520 | tf_op jit(solution)/shard_map/ghqk,gqhc->gkhc/dot_general | solution.py:139
  336.3 9.9 %select_convert_fusion.3 = (bf16[1,3,64,640]{3,2,1,0:T(8,128)(2,1)}, bf16[1,3,64,640]{3,2,1,0:T(8,128)(2,1)}, bf16[1,3,64,640]{3,2,1,0:T(8,128)(2,1)}, bf16[1,3,64,640]{3,2,1,0:T(8,128)(2,1)}) fusion(pred[640]{0:T(1024)(128)(4,1)S(1)} %compare_reduce_fusion, bf16[1,3,64,640]{3,2,1,0:T(8,128)(2,1)} %convolution_bitcast_fusion.4, ...), kind=kOutput, calls=%fused_computation.79 | convolution fusion | flops 167610880 | bytes 11313280 | tf_op jit(solution)/shard_map/ghqk,gkhc->gqhc/dot_general | solution.py:131
  347.8 3.6 fusion.12
  351.6 3.9 convolution_bitcast_fusion
  355.4 4.5 copy.56
  359.9 4.7 reshape.293
  366.0 2.2 copy.60
  368.3 2.2 convolution_bitcast_fusion.3
  370.4 2.3 copy.58
  372.8 4.2 fusion.64
  378.3 2.8 fusion.44
  381.1 24.7 %all-reduce = (f32[768]{0:T(1024)}, f32[768]{0:T(1024)}, f32[768]{0:T(1024)}, f32[768]{0:T(1024)}, f32[768]{0:T(1024)}, /*index=5*/f32[768]{0:T(1024)}, f32[768]{0:T(1024)}) all-reduce(f32[768]{0:T(1024)S(1)} %get-tuple-element.59, f32[768]{0:T(1024)S(1)} %get-tuple-element.45, ...), channel_id=1, replica_groups=mesh['dp'=8,'mp'=4] {'dp'}, use_global_device_ids=true, to_apply=%region_20.21 | all-reduce | flops 5376 | bytes 43008 | tf_op jit(solution)/shard_map/psum | solution.py:180
  408.6 19.8 %all_gather.11 = bf16[640,768]{1,0:T(8,128)(2,1)S(1)} all-gather(bf16[160,768]{1,0:T(8,128)(2,1)S(1)} %add_convert_fusion.2), channel_id=1, replica_groups=mesh['dp'=8,'mp'=4] {'mp'}, dimensions={0}, use_global_device_ids=true | all-gather | bytes 1228800 | tf_op jit(solution)/shard_map/all_gather | solution.py:171
  428.5 4.0 reduce-scatter.22.cloned.1.call-done
  434.5 36.6 %reduce-scatter.26.cloned.1.call-done = f32[96,192]{1,0:T(8,128)} async-done(((f32[768,192]{1,0:T(8,128)}), f32[96,192]{1,0:T(8,128)}) %reduce-scatter.26.cloned.1.call-update) | async-done | bytes 73744
  471.1 38.7 %reduce-scatter.24.cloned.1.call-done = f32[96,192]{1,0:T(8,128)} async-done(((f32[768,192]{1,0:T(8,128)}), f32[96,192]{1,0:T(8,128)}) %reduce-scatter.24.cloned.1.call-update) | async-done | bytes 73744
  509.8 46.3 %reduce-scatter.20.cloned.1.call-done = f32[768,96]{0,1:T(8,128)} async-done(((f32[768,768]{0,1:T(8,128)}), f32[768,96]{0,1:T(8,128)}) %reduce-scatter.20.cloned.1.call-update) | async-done | bytes 294928 | tf_op jit(solution)/shard_map/reduce_scatter | solution.py:178
  556.2 46.1 %reduce-scatter.18.cloned.1.call-done = f32[96,768]{1,0:T(8,128)} async-done(((f32[768,768]{1,0:T(8,128)}), f32[96,768]{1,0:T(8,128)}) %reduce-scatter.18.cloned.1.call-update) | async-done | bytes 294928 | tf_op jit(solution)/shard_map/reduce_scatter | solution.py:177
  (150 shorter events, 40.0 us)
Async XLA Ops:
  7.2 166.6 %copy-start = (bf16[768,768]{1,0:T(8,128)(2,1)S(1)}, bf16[768,768]{1,0:T(8,128)(2,1)}, u32[]{:S(2)}) copy-start(bf16[768,768]{1,0:T(8,128)(2,1)} %param.27) | copy-start | bytes 3538948
  7.2 4.8 copy-start.3
  7.2 4.5 copy-start.33
  7.2 158.7 %all-gather.3.cloned.1.call-start = ((), (), s32[]{:S(2)}) async-start(), calls=%async_computation.12 | async-start | bytes 9830400 | tf_op jit(solution)/shard_map/all_gather | solution.py:86
  9.8 5.6 copy-start.10
  11.7 6.1 copy-start.12
  22.0 209.6 %all-reduce.4.cloned.1.call-start = ((), (), s32[]{:S(2)}) async-start(), calls=%async_computation.7 | async-start | bytes 1966080 | tf_op jit(solution)/shard_map/psum | solution.py:94
  166.0 5.3 copy-start.29
  174.1 7.4 %copy-start.34 = (bf16[768,768]{1,0:T(8,128)(2,1)S(1)}, bf16[768,768]{1,0:T(8,128)(2,1)}, u32[]{:S(2)}) copy-start(bf16[768,768]{1,0:T(8,128)(2,1)} %param.29) | copy-start | bytes 3538948
  181.5 50.1 %copy-start.30 = (f32[768]{0:T(1024)S(1)}, f32[768]{0:T(1024)}, u32[]{:S(2)}) copy-start(f32[768]{0:T(1024)} %param.30) | copy-start | bytes 9220
  183.4 108.7 %all-reduce.6.cloned.1.call-start = ((), (), s32[]{:S(2)}) async-start(), calls=%async_computation.8 | async-start | bytes 1966080 | tf_op jit(solution)/shard_map/psum | solution.py:107
  235.6 2.9 copy-start.44
  237.5 2.6 copy-start.6
  243.0 162.8 %reduce-scatter.28.cloned.1.call-start = ((), (), s32[]{:S(2)}) async-start(), calls=%async_computation.16 | async-start | bytes 884736
  292.2 3.1 copy-start.7
  292.2 3.1 copy-start.8
  299.3 3.4 copy-start.13
  302.6 3.1 copy-start.24
  302.7 3.1 copy-start.26
  305.7 9.7 %copy-start.11 = (bf16[640,192]{0,1:T(8,128)(2,1)S(1)}, bf16[640,192]{0,1:T(8,128)(2,1)}, u32[]{:S(2)}) copy-start(bf16[640,192]{0,1:T(8,128)(2,1)} %copy-done.10) | copy-start | bytes 737284
  315.4 9.8 %copy-start.17 = (bf16[768,192]{0,1:T(8,128)(2,1)S(1)}, bf16[768,192]{0,1:T(8,128)(2,1)}, u32[]{:S(2)}) copy-start(bf16[768,192]{0,1:T(8,128)(2,1)} %param.22) | copy-start | bytes 884740
  325.0 82.4 %reduce-scatter.16.cloned.1.call-start = ((), (), s32[]{:S(2)}) async-start(), calls=%async_computation.9 | async-start | bytes 1228800 | tf_op jit(solution)/shard_map/reduce_scatter | solution.py:162
  336.3 10.0 %copy-start.19 = (bf16[3,64,640]{2,1,0:T(8,128)(2,1)}, bf16[3,64,640]{2,1,0:T(8,128)(2,1)S(1)}, u32[]{:S(2)}) copy-start(bf16[3,64,640]{2,1,0:T(8,128)(2,1)S(1)} %fusion.20) | copy-start | bytes 737284
  336.3 10.0 %copy-start.18 = (bf16[768,192]{0,1:T(8,128)(2,1)S(1)}, bf16[768,192]{0,1:T(8,128)(2,1)}, u32[]{:S(2)}) copy-start(bf16[768,192]{0,1:T(8,128)(2,1)} %param.21) | copy-start | bytes 884740
  347.8 3.7 copy-start.4
  351.5 80.9 %reduce-scatter.22.cloned.1.call-start = ((), (), s32[]{:S(2)}) async-start(), calls=%async_computation.13 | async-start | bytes 2654208
  364.7 106.4 %reduce-scatter.26.cloned.1.call-start = ((), (), s32[]{:S(2)}) async-start(), calls=%async_computation.15 | async-start | bytes 884736
  368.2 141.6 %reduce-scatter.24.cloned.1.call-start = ((), (), s32[]{:S(2)}) async-start(), calls=%async_computation.14 | async-start | bytes 884736
  370.4 2.4 copy-start.40
  372.8 183.4 %reduce-scatter.20.cloned.1.call-start = ((), (), s32[]{:S(2)}) async-start(), calls=%async_computation.11 | async-start | bytes 2654208 | tf_op jit(solution)/shard_map/reduce_scatter | solution.py:178
  377.1 225.2 %reduce-scatter.18.cloned.1.call-start = ((), (), s32[]{:S(2)}) async-start(), calls=%async_computation.10 | async-start | bytes 2654208 | tf_op jit(solution)/shard_map/reduce_scatter | solution.py:177
  408.6 194.6 %copy-start.1 = (bf16[768,768]{1,0:T(8,128)(2,1)S(1)}, bf16[768,768]{1,0:T(8,128)(2,1)}, u32[]{:S(2)}) copy-start(bf16[768,768]{1,0:T(8,128)(2,1)} %param.27) | copy-start | bytes 3538948
  (23 other events, 28.9 us)
Sparse Core Ops, SparseCore 0:
  22.2 143.7 all-gather.2
  183.5 48.0 all-reduce.3
  243.1 49.0 all-reduce.5
  325.1 34.1 reduce-scatter.27
  362.0 26.2 reduce-scatter.15
  391.5 40.8 reduce-scatter.21
  436.2 34.9 reduce-scatter.25
  474.8 34.9 reduce-scatter.23
  513.8 42.3 reduce-scatter.19
  559.9 42.3 reduce-scatter.17
